TPU v7x, 32 devices: a whole 2x2x4 slice. The times are simulated.
32 devices in a mesh: dp: 2 (over y), pipe: 4 (over x, core), tensor: 4 (over z).
Axes of the slice: x: 2, y: 2, z: 4, core: 2. Of those that a mesh axis runs over, the one named last changes fastest.
Arguments:
- query_states: bfloat16 [4, 512, 1024], P('dp'), may hold values from -6 to 6
- doc_states: bfloat16 [4, 512, 1024], P('dp'), may hold values from -6 to 6
- query_len: int32 [4], P('dp'), may hold values from 64 to 512
- doc_len: int32 [4], P('dp'), may hold values from 64 to 512
- doc_order: int32 [2, 2], P('dp'), may hold values from 0 to 1, each once within a row
- w_qkv: bfloat16 [4, 3, 1024, 1024], P('pipe', None, None, 'tensor'), may hold values from -0.1875 to 0.1875
- w_out: bfloat16 [4, 1024, 1024], P('pipe', 'tensor'), may hold values from -0.1875 to 0.1875
- w_up: bfloat16 [4, 1024, 4096], P('pipe', None, 'tensor'), may hold values from -0.1875 to 0.1875
- w_down: bfloat16 [4, 4096, 1024], P('pipe', 'tensor'), may hold values from -0.09375 to 0.09375
- gain_attn: float32 [4, 1024], P('pipe'), may hold values from 0.1 to 1.9
- gain_mlp: float32 [4, 1024], P('pipe'), may hold values from 0.1 to 1.9
Outputs:
- query_vectors: bfloat16 [4, 1024], P('dp', ('pipe', 'tensor'))
- document_vectors: bfloat16 [4, 1024], P('dp', ('pipe', 'tensor'))
- pair_loss: float32 [4], P('dp')
Inputs may be any that keep to these rules, and one draw needn't show every extreme that they name: `doc_order`: each row holds every number of 0 to 1 once.
All inputs are finite; a program needn't handle non-finite values.
Results may differ from a plain program's by a relative error of at most 0.035.
Values may be sent and summed in bfloat16 or wider, within the bound.
No kernel may reach another device: no remote copies, remote signals or barrier semaphores. Data moves between devices by JAX's collectives and lax.ppermute only.
A program may use at most 192 MiB of HBM per device.

v0:
```python
import functools
import math

import jax
import jax.numpy as jnp
from jax import lax
from jax.experimental import pallas as pl
from jax.experimental.pallas import tpu as pltpu
from jax.sharding import PartitionSpec as P

HEAD_WIDTH = 64
LANES = 128
SOFTMAX_TEMPER = 0.05
EPSILON = 1e-06
LAYER_EPSILON = 1e-12


def norm_rows(values_in, gain_row):
    row_mean = jnp.mean(values_in, axis=-1, keepdims=True)
    centered = values_in - row_mean
    variance = jnp.mean(centered * centered, axis=-1, keepdims=True)
    return centered * lax.rsqrt(variance + LAYER_EPSILON) * gain_row


def gelu(x):
    return 0.5 * x * (1.0 + lax.erf(x * math.sqrt(0.5)))


def start_attention_weights(group, refs, w_in, w_ctx, sems):
    groups = w_in.shape[0]
    width = w_ctx.shape[1]
    offset = 0
    if len(refs) == 2 and refs[0].shape[0] == 3:
        members = [(refs[0], lambda column: refs[1].at[:, column], width)]
    else:
        members = [
            (ref, lambda column, ref=ref: ref.at[3, column, :], ref.shape[2]) for ref in refs
        ]
    for qkv, ctx_block, part in members:
        for kind in range(3):
            pltpu.make_async_copy(
                qkv.at[kind],
                w_in.at[group, :, pl.ds(kind * width + offset, part)],
                sems.at[group],
            ).start()
        for start in range(0, w_ctx.shape[2], part):
            pltpu.make_async_copy(
                ctx_block(pl.ds(start, part)),
                w_ctx.at[group, pl.ds(offset, part), pl.ds(start, part)],
                sems.at[groups + group],
            ).start()
        offset += part


def attention_kernel(slot, shares, source_count, plan, *refs):
    query_ref, doc_ref = refs[:2]
    passed_refs = refs[2 : 2 + source_count]
    weight_refs = refs[2 + source_count : -7]
    gain_ref, out_ref, hidden, w_in, w_ctx, total, sems = refs[-7:]
    groups = w_in.shape[0]
    width = w_ctx.shape[1]
    pairs_here = query_ref.shape[0]
    slot_count = hidden.shape[0]

    @pl.when(plan[slot, 0] == 1)
    def _():
        source = plan[slot, 2]
        entry = plan[slot, 3]
        hidden_sem = sems.at[2 * groups]

        @pl.when((source == 0) & (entry < pairs_here))
        def _():
            pltpu.make_async_copy(
                query_ref.at[jnp.minimum(entry, pairs_here - 1)], hidden, hidden_sem
            ).start()

        @pl.when((source == 0) & (entry >= pairs_here))
        def _():
            pltpu.make_async_copy(
                doc_ref.at[jnp.clip(entry - pairs_here, 0, pairs_here - 1)], hidden, hidden_sem
            ).start()

        for tag, ref in zip((1, 2), passed_refs):

            @pl.when(source == tag)
            def _(ref=ref):
                pltpu.make_async_copy(ref, hidden, hidden_sem).start()

        for group, members in enumerate(shares):
            start_attention_weights(
                group, [weight_refs[member] for member in members], w_in, w_ctx, sems
            )
        pltpu.make_async_copy(query_ref.at[0], hidden, hidden_sem).wait()
        valid = lax.broadcasted_iota(jnp.int32, (1, slot_count), 1) < plan[slot, 1]
        low_lanes = lax.broadcasted_iota(jnp.int32, (1, LANES), 1) < HEAD_WIDTH
        total[...] = hidden[...].astype(jnp.float32)

        def one_group(group, carry):
            pltpu.make_async_copy(w_in.at[group], w_in.at[group], sems.at[group]).wait()
            pltpu.make_async_copy(w_ctx.at[group], w_ctx.at[group], sems.at[groups + group]).wait()
            rows = jnp.dot(hidden[...], w_in[group], preferred_element_type=jnp.float32)
            queries = (rows[:, :width] * (1.0 / math.sqrt(HEAD_WIDTH))).astype(jnp.bfloat16)
            keys = rows[:, width : 2 * width].astype(jnp.bfloat16)
            values = rows[:, 2 * width :].astype(jnp.bfloat16)
            contexts = []
            for start in range(0, width, LANES):
                q2, k2, v2 = (a[:, start : start + LANES] for a in (queries, keys, values))
                halves = []
                for keep in (low_lanes, ~low_lanes):
                    q1 = jnp.where(keep, q2, jnp.zeros_like(q2))
                    scores = lax.dot_general(
                        q1, k2, (((1,), (1,)), ((), ())), preferred_element_type=jnp.float32
                    )
                    exps = jnp.where(valid, jnp.exp(scores), 0.0)
                    share = 1.0 / jnp.sum(exps, axis=-1, keepdims=True)
                    attention = (exps * share).astype(jnp.bfloat16)
                    halves.append(jnp.dot(attention, v2, preferred_element_type=jnp.float32))
                contexts.append(jnp.where(low_lanes, halves[0], halves[1]).astype(jnp.bfloat16))
            context = jnp.concatenate(contexts, axis=1)
            total[...] += jnp.dot(context, w_ctx[group], preferred_element_type=jnp.float32)
            return carry

        lax.fori_loop(0, groups, one_group, 0)
        out_ref[...] = norm_rows(total[...], gain_ref[...]).astype(jnp.bfloat16)


def attention_half(slot, plan, queries, docs, passed, weights, shares, gain):
    _, slot_count, model_width = queries.shape
    groups = len(shares)
    width = weights[1].shape[0]
    far = pl.BlockSpec(memory_space=pltpu.HBM)
    near = pl.BlockSpec(memory_space=pltpu.VMEM)
    return pl.pallas_call(
        functools.partial(attention_kernel, slot, shares, len(passed)),
        out_shape=jax.ShapeDtypeStruct((slot_count, model_width), jnp.bfloat16),
        in_specs=[pl.BlockSpec(memory_space=pltpu.SMEM)]
        + [far] * (2 + len(passed) + len(weights))
        + [near],
        out_specs=near,
        scratch_shapes=[
            pltpu.VMEM((slot_count, model_width), jnp.bfloat16),
            pltpu.VMEM((groups, model_width, 3 * width), jnp.bfloat16),
            pltpu.VMEM((groups, width, model_width), jnp.bfloat16),
            pltpu.VMEM((slot_count, model_width), jnp.float32),
            pltpu.SemaphoreType.DMA((2 * groups + 1,)),
        ],
        compiler_params=pltpu.CompilerParams(vmem_limit_bytes=40 * 2**20),
        name="attention_half",
    )(plan, queries, docs, *passed, *weights, gain)


def mlp_kernel(slot, plan, hidden, *refs):
    weight_refs = refs[:-7]
    gain_ref, out_ref, pool_ref, w_up, w_down, total, sems = refs[-7:]
    chunks = w_up.shape[0]
    chunk_width = w_up.shape[2]

    @pl.when(plan[slot, 0] == 1)
    def _():
        index = 0
        for member in range(len(weight_refs) // 2):
            up_ref, down_ref = weight_refs[2 * member], weight_refs[2 * member + 1]
            for start in range(0, down_ref.shape[0], chunk_width):
                pltpu.make_async_copy(
                    up_ref.at[:, pl.ds(start, chunk_width)], w_up.at[index], sems.at[index]
                ).start()
                pltpu.make_async_copy(
                    down_ref.at[pl.ds(start, chunk_width), :],
                    w_down.at[index],
                    sems.at[chunks + index],
                ).start()
                index += 1
        total[...] = hidden[...].astype(jnp.float32)

        def one_chunk(chunk, carry):
            pltpu.make_async_copy(w_up.at[chunk], w_up.at[chunk], sems.at[chunk]).wait()
            pltpu.make_async_copy(w_down.at[chunk], w_down.at[chunk], sems.at[chunks + chunk]).wait()
            before = jnp.dot(hidden[...], w_up[chunk], preferred_element_type=jnp.float32)
            total[...] += jnp.dot(
                gelu(before).astype(jnp.bfloat16),
                w_down[chunk],
                preferred_element_type=jnp.float32,
            )
            return carry

        lax.fori_loop(0, chunks, one_chunk, 0)
        result = norm_rows(total[...], gain_ref[...]).astype(jnp.bfloat16)
        out_ref[...] = result
        used = lax.broadcasted_iota(jnp.int32, (result.shape[0], 1), 0) < plan[slot, 1]
        pool_ref[...] = jnp.sum(
            jnp.where(used, result.astype(jnp.float32), 0.0), axis=0, keepdims=True
        )


def mlp_half(slot, plan, hidden, weights, gain):
    slot_count, model_width = hidden.shape
    chunk_width = min(down.shape[0] for down in weights[1::2])
    chunks = sum(down.shape[0] for down in weights[1::2]) // chunk_width
    far = pl.BlockSpec(memory_space=pltpu.HBM)
    near = pl.BlockSpec(memory_space=pltpu.VMEM)
    return pl.pallas_call(
        functools.partial(mlp_kernel, slot),
        out_shape=(
            jax.ShapeDtypeStruct((slot_count, model_width), jnp.bfloat16),
            jax.ShapeDtypeStruct((1, model_width), jnp.float32),
        ),
        in_specs=[pl.BlockSpec(memory_space=pltpu.SMEM), near] + [far] * len(weights) + [near],
        out_specs=(near, near),
        scratch_shapes=[
            pltpu.VMEM((chunks, model_width, chunk_width), jnp.bfloat16),
            pltpu.VMEM((chunks, chunk_width, model_width), jnp.bfloat16),
            pltpu.VMEM((slot_count, model_width), jnp.float32),
            pltpu.SemaphoreType.DMA((2 * chunks,)),
        ],
        compiler_params=pltpu.CompilerParams(vmem_limit_bytes=48 * 2**20),
        name="mlp_half",
    )(plan, hidden, *weights, gain)


def half_shard(w_qkv, w_out, w_up, w_down, which):
    def cut(piece, dim):
        size = piece.shape[dim] // 2
        return lax.dynamic_slice_in_dim(piece, which * size, size, dim)

    qkv, out = cut(w_qkv, 2), cut(w_out, 0)
    part, width = out.shape
    blocks = out.reshape(part, width // part, part).swapaxes(0, 1).reshape(1, width, part)
    return [jnp.concatenate([qkv, blocks], axis=0), cut(w_up, 1), cut(w_down, 0)]


def per_device(
    query_states,
    doc_states,
    query_len,
    doc_len,
    doc_order,
    w_qkv,
    w_out,
    w_up,
    w_down,
    gain_attn,
    gain_mlp,
):
    pair_count, _, model_width = query_states.shape
    seq_count = 2 * pair_count
    dp_count = lax.axis_size("dp")
    dp_index = lax.axis_index("dp")
    section_count = lax.axis_size("pipe")
    section = lax.axis_index("pipe")
    tensor_count = lax.axis_size("tensor")
    tensor_index = lax.axis_index("tensor")
    side = tensor_count // 2
    batch = seq_count // 2

    shared = dp_count % 2 == 0
    parity = dp_index % 2 if shared else 0
    mine = (w_qkv[0], w_out[0], w_up[0], w_down[0])
    own_first, own_second = (half_shard(*mine, which) for which in (parity, 1 - parity))
    across = [(side - 1, side), (side, side - 1)]
    swap = [(index, index ^ 1) for index in range(dp_count)]

    inwards = [[(side - 1 - step, side - 1), (side + step, side)] for step in range(1, side)]
    kinds = len(own_first)
    firsts = [own_first] + [[] for _ in inwards]
    seconds = [own_second] + [[] for _ in inwards]
    crossed = [[] for _ in firsts]
    swapped = [[] for _ in firsts]
    for kind in range(kinds):
        for index, pairs in enumerate(inwards):
            firsts[index + 1].append(lax.ppermute(own_first[kind], "tensor", pairs))
        crossed[0].append(lax.ppermute(own_first[kind], "tensor", across))
    for kind in range(kinds):
        for index, pairs in enumerate(inwards):
            seconds[index + 1].append(lax.ppermute(own_second[kind], "tensor", pairs))

    def pass_on(index, kind):
        if shared:
            swapped[index].append(lax.ppermute(crossed[index][kind], "dp", swap))
        else:
            swapped[index].append(lax.ppermute(seconds[index][kind], "tensor", across))

    for kind in range(kinds):
        for index in range(1, side):
            crossed[index].append(lax.ppermute(firsts[index][kind], "tensor", across))
        pass_on(0, kind)
        if kind > 0:
            for index in range(1, side):
                pass_on(index, kind - 1)
    for index in range(1, side):
        pass_on(index, kinds - 1)
    halves = []
    for index in range(1, side):
        halves += [firsts[index], seconds[index]]
    for index in range(side):
        halves += [crossed[index], swapped[index]]
    attention_weights = [mine[0], mine[1]] + [half[0] for half in halves]
    groups = [(0, 1)] + [(2 + i, 3 + i) for i in range(0, len(halves), 2)]
    mlp_weights = [mine[2], mine[3]] + [piece for half in halves for piece in half[1:]]

    lengths = jnp.concatenate([query_len, doc_len])
    host = jnp.clip(tensor_index - (side - 1), 0, 1)
    is_host = (tensor_index == side - 1) | (tensor_index == side)

    def lag(index):
        return index + index // 2

    slots = lag(section_count - 1) + batch
    steps = jnp.arange(slots, dtype=jnp.int32)
    local = steps - lag(section)
    active = (local >= 0) & (local < batch) & is_host
    entry = host * batch + jnp.clip(local, 0, batch - 1)
    picks = entry[:, None] == jnp.arange(seq_count, dtype=jnp.int32)[None, :]
    slot_lengths = jnp.sum(jnp.where(picks, lengths[None, :], 0), axis=1)
    source = jnp.where(section == 0, 0, jnp.where(section % 2 == 1, 1, 2))
    plan = jnp.stack(
        [active.astype(jnp.int32), slot_lengths, jnp.full_like(steps, source), entry], axis=1
    ).astype(jnp.int32)
    fast, slow, sums = {}, {}, []
    for slot in range(slots):
        passed = [
            fast.get(slot - 1, query_states[0]),
            slow.get(slot - 2, query_states[0]),
        ]
        mixed = attention_half(
            slot, plan, query_states, doc_states, passed, attention_weights, groups, gain_attn
        )
        hidden, pool = mlp_half(slot, plan, mixed, mlp_weights, gain_mlp)
        sums.append(pool)
        for step, table in ((0, fast), (1, slow)):
            moves = [
                (index, index + 1)
                for index in range(step, section_count - 1, 2)
                if 0 <= slot - lag(index) < batch
            ]
            if moves:
                table[slot] = lax.ppermute(hidden, "pipe", moves)

    summed = jnp.concatenate(sums[slots - batch :], axis=0)
    own_lengths = lax.dynamic_slice_in_dim(lengths, host * batch, batch, 0)
    pooled = summed / own_lengths.astype(jnp.float32)[:, None]
    embedded = (
        pooled * lax.rsqrt(jnp.sum(pooled * pooled, axis=1, keepdims=True) + EPSILON)
    ).astype(jnp.bfloat16)
    embedded = jnp.where(is_host & (section == section_count - 1), embedded, jnp.zeros_like(embedded))
    table = lax.psum(lax.all_gather(embedded, "dp"), "pipe")
    table = jnp.where(
        jnp.arange(2, dtype=jnp.int32)[None, :, None, None] == host,
        table[:, None],
        jnp.zeros_like(table)[:, None],
    )
    table = lax.psum(table, "tensor").astype(jnp.bfloat16)
    table = table.reshape(dp_count, seq_count, model_width)
    mine = lax.dynamic_index_in_dim(table, dp_index, 0, keepdims=False)
    local_queries, local_docs = mine[:pair_count], mine[pair_count:]
    all_docs = table[:, pair_count:].reshape(dp_count * pair_count, model_width)
    scores = (
        lax.dot_general(
            local_queries,
            all_docs,
            (((1,), (1,)), ((), ())),
            preferred_element_type=jnp.float32,
        )
        / SOFTMAX_TEMPER
    )
    columns = jnp.arange(dp_count * pair_count, dtype=jnp.int32)
    positive = dp_index * pair_count + doc_order[0]
    positive_score = jnp.sum(
        jnp.where(columns[None, :] == positive[:, None], scores, 0.0), axis=1
    )
    pair_loss = jnp.log(jnp.sum(jnp.exp(scores), axis=1)) - positive_score
    piece_width = model_width // (section_count * tensor_count)
    first = (section * tensor_count + tensor_index) * piece_width
    return (
        lax.dynamic_slice_in_dim(local_queries, first, piece_width, 1),
        lax.dynamic_slice_in_dim(local_docs, first, piece_width, 1),
        pair_loss,
    )


def solution(mesh):
    in_specs = (
        P("dp", None, None),
        P("dp", None, None),
        P("dp"),
        P("dp"),
        P("dp", None),
        P("pipe", None, None, "tensor"),
        P("pipe", "tensor", None),
        P("pipe", None, "tensor"),
        P("pipe", "tensor", None),
        P("pipe", None),
        P("pipe", None),
    )
    out_specs = (P("dp", ("pipe", "tensor")), P("dp", ("pipe", "tensor")), P("dp"))
    return jax.shard_map(
        per_device, mesh=mesh, in_specs=in_specs, out_specs=out_specs, check_vma=False
    )
```

profile of v0, /device:TPU:0, one launch (start us, length us, event | category | flops | bytes accessed | tf_op | source)
XLA Modules:
  0.0 433.6 jit_solution(11764018323223288510)
XLA Ops:
  5.3 8.7 %collective-permute-start = (bf16[4,1024,128]{2,1,0:T(8,128)(2,1)}, bf16[4,1024,128]{2,1,0:T(8,128)(2,1)}, u32[]{:S(2)}, u32[]{:S(2)}) collective-permute-start(bf16[4,1024,128]{2,1,0:T(8,128)(2,1)} %pad_maximum_fusion), channel_id=1, source_target_pairs={{0,1},{3,2},{4,5},{7,6},{8,9},{11,10},{12,13},{15,14},{16,17},{19,... | collective-permute-start | bytes 3145736 | tf_op jit(solution)/shard_map/ppermute | solution.py:270
  16.0 2.2 pad_maximum_fusion.1
  18.2 2.3 collective-permute-start.1
  24.7 13.9 %collective-permute-start.6 = (bf16[1024,512]{1,0:T(8,128)(2,1)S(1)}, bf16[1024,512]{1,0:T(8,128)(2,1)}, u32[]{:S(2)}, u32[]{:S(2)}) collective-permute-start(bf16[1024,512]{1,0:T(8,128)(2,1)S(1)} %get-tuple-element.22), channel_id=1, source_target_pairs={{0,1},{3,2},{4,5},{7,6},{8,9},{11,10},{12,13},{15,14},{16,17},{19,... | collective-permute-start | bytes 3145736 | tf_op jit(solution)/shard_map/ppermute | solution.py:270
  38.7 3.6 collective-permute-start.7
  42.3 17.1 %collective-permute-done.1.refs_7_ = bf16[4,1024,128]{2,1,0:T(8,128)(2,1)} collective-permute-done((bf16[4,1024,128]{2,1,0:T(8,128)(2,1)}, bf16[4,1024,128]{2,1,0:T(8,128)(2,1)}, u32[]{:S(2)}, u32[]{:S(2)}) %collective-permute-start.1) | collective-permute-done | bytes 1048608 | tf_op jit(solution)/shard_map/ppermute | solution.py:274
  61.0 20.7 %collective-permute-done.8.refs_4_ = bf16[1024,512]{1,0:T(8,128)(2,1)S(1)} collective-permute-done((bf16[1024,512]{1,0:T(8,128)(2,1)S(1)}, bf16[1024,512]{1,0:T(8,128)(2,1)S(1)}, u32[]{:S(2)}, u32[]{:S(2)}) %collective-permute-start.8) | collective-permute-done | bytes 1048608 | tf_op jit(solution)/shard_map/ppermute | solution.py:274
  86.9 17.3 %collective-permute-done.6.refs_2_ = bf16[1024,512]{1,0:T(8,128)(2,1)} collective-permute-done((bf16[1024,512]{1,0:T(8,128)(2,1)S(1)}, bf16[1024,512]{1,0:T(8,128)(2,1)}, u32[]{:S(2)}, u32[]{:S(2)}) %collective-permute-start.6) | collective-permute-done | bytes 1048608 | tf_op jit(solution)/shard_map/ppermute | solution.py:270
  105.8 19.5 %collective-permute-done.7.refs_3_ = bf16[512,1024]{1,0:T(8,128)(2,1)} collective-permute-done((bf16[512,1024]{1,0:T(8,128)(2,1)}, bf16[512,1024]{1,0:T(8,128)(2,1)}, u32[]{:S(2)}, u32[]{:S(2)}) %collective-permute-start.7) | collective-permute-done | bytes 1048608 | tf_op jit(solution)/shard_map/ppermute | solution.py:270
  128.7 6.1 %collective-permute-start.9 = (bf16[512,1024]{1,0:T(8,128)(2,1)}, bf16[512,1024]{1,0:T(8,128)(2,1)}, u32[]{:S(2)}, u32[]{:S(2)}) collective-permute-start(bf16[512,1024]{1,0:T(8,128)(2,1)} %get-tuple-element.19), channel_id=1, source_target_pairs={{0,1},{3,2},{4,5},{7,6},{8,9},{11,10},{12,13},{15,14},{16,17},{19,... | collective-permute-start | bytes 3145736 | tf_op jit(solution)/shard_map/ppermute | solution.py:274
  137.3 16.1 %collective-permute-done.5.refs_11_ = bf16[4,1024,128]{2,1,0:T(8,128)(2,1)} collective-permute-done((bf16[4,1024,128]{2,1,0:T(8,128)(2,1)}, bf16[4,1024,128]{2,1,0:T(8,128)(2,1)}, u32[]{:S(2)}, u32[]{:S(2)}) %collective-permute-start.5) | collective-permute-done | bytes 1048608 | tf_op jit(solution)/shard_map/ppermute | solution.py:278
  158.7 17.2 %collective-permute-done.12.refs_8_ = bf16[1024,512]{1,0:T(8,128)(2,1)} collective-permute-done((bf16[1024,512]{1,0:T(8,128)(2,1)}, bf16[1024,512]{1,0:T(8,128)(2,1)}, u32[]{:S(2)}, u32[]{:S(2)}) %collective-permute-start.12) | collective-permute-done | bytes 1048608 | tf_op jit(solution)/shard_map/ppermute | solution.py:278
  175.9 22.5 %collective-permute-done.13.refs_9_ = bf16[512,1024]{1,0:T(8,128)(2,1)} collective-permute-done((bf16[512,1024]{1,0:T(8,128)(2,1)}, bf16[512,1024]{1,0:T(8,128)(2,1)}, u32[]{:S(2)}, u32[]{:S(2)}) %collective-permute-start.13) | collective-permute-done | bytes 1048608 | tf_op jit(solution)/shard_map/ppermute | solution.py:278
  198.4 22.5 %collective-permute-done.16.refs_12_ = bf16[1024,512]{1,0:T(8,128)(2,1)} collective-permute-done((bf16[1024,512]{1,0:T(8,128)(2,1)}, bf16[1024,512]{1,0:T(8,128)(2,1)}, u32[]{:S(2)}, u32[]{:S(2)}) %collective-permute-start.16) | collective-permute-done | bytes 1048608 | tf_op jit(solution)/shard_map/ppermute | solution.py:278
  220.9 20.2 %collective-permute-done.17.refs_13_ = bf16[512,1024]{1,0:T(8,128)(2,1)} collective-permute-done((bf16[512,1024]{1,0:T(8,128)(2,1)}, bf16[512,1024]{1,0:T(8,128)(2,1)}, u32[]{:S(2)}, u32[]{:S(2)}) %collective-permute-start.17) | collective-permute-done | bytes 1048608 | tf_op jit(solution)/shard_map/ppermute | solution.py:278
  243.8 2.2 collective-permute-done.18.refs_2_
  246.0 7.2 %attention_half.7.hidden = bf16[512,1024]{1,0:T(8,128)(2,1)S(1)} custom-call(s32[6,4]{1,0:T(8,128)S(1)} %pad_add_fusion.plan, bf16[2,512,1024]{2,1,0:T(8,128)(2,1)S(1)} %copy-done, bf16[2,512,1024]{2,1,0:T(8,128)(2,1)} %refs_1_.11, bf16[512,1024]{1,0:T(8,128)(2,1)S(1)} %collective-permute-done.18.refs_2_, ...), custom_call_target="tpu_custom_call" | custom-call | tf_op jit(solution)/shard_map/attention_half/pallas_call | solution.py:133
  254.6 2.3 collective-permute-start.21
  262.4 7.1 %attention_half.8.hidden = bf16[512,1024]{1,0:T(8,128)(2,1)S(1)} custom-call(s32[6,4]{1,0:T(8,128)S(1)} %pad_add_fusion.plan, bf16[2,512,1024]{2,1,0:T(8,128)(2,1)S(1)} %copy-done, bf16[2,512,1024]{2,1,0:T(8,128)(2,1)} %refs_1_.11, bf16[512,1024]{1,0:T(8,128)(2,1)S(1)} %slice_bitcast_fusion.refs_2_.refs_3_, ...), custom_call_target="tpu_custom_call" | custom-call | tf_op jit(solution)/shard_map/attention_half/pallas_call | solution.py:133
  272.3 1.8 mlp_half.10
  279.5 3.4 attention_half.11.hidden
  285.0 4.4 %all_gather.4 = bf16[2,2,1024]{2,1,0:T(2,128)(2,1)S(1)} all-gather(bf16[1,2,1024]{2,1,0:T(2,128)(2,1)S(1)} %broadcast_select_fusion.1), channel_id=1, replica_groups=mesh['dp'=2,'pipe'=4,'tensor'=4] {'dp'}, dimensions={0}, use_global_device_ids=true | all-gather | bytes 12288 | tf_op jit(solution)/shard_map/all_gather | solution.py:345
  289.3 19.8 %psum.14 = bf16[2,2,1024]{2,1,0:T(2,128)(2,1)S(1)} all-reduce(bf16[2,2,1024]{2,1,0:T(2,128)(2,1)S(1)} %all_gather.4), channel_id=1, replica_groups=mesh['dp'=2,'pipe'=4,'tensor'=4] {'pipe'}, use_global_device_ids=true, to_apply=%region_2.3 | all-reduce | flops 4096 | bytes 16384 | tf_op jit(solution)/shard_map/psum | solution.py:345
  309.3 122.7 %psum.15 = bf16[2,4,1024]{2,1,0:T(4,128)(2,1)S(1)} all-reduce(bf16[2,4,1024]{2,1,0:T(4,128)(2,1)S(1)} %reshape.167), channel_id=1, replica_groups=mesh['dp'=2,'pipe'=4,'tensor'=4] {'tensor'}, use_global_device_ids=true, to_apply=%region_3.4 | all-reduce | flops 8192 | bytes 32768 | tf_op jit(solution)/shard_map/psum | solution.py:351
  (113 shorter events, 51.4 us)
Async XLA Ops:
  4.5 20.3 %collective-permute-start.2 = (bf16[4,1024,128]{2,1,0:T(8,128)(2,1)}, bf16[4,1024,128]{2,1,0:T(8,128)(2,1)S(1)}, u32[]{:S(2)}, u32[]{:S(2)}) collective-permute-start(bf16[4,1024,128]{2,1,0:T(8,128)(2,1)} %pad_maximum_fusion), channel_id=1, source_target_pairs={{1,2},{2,1},{5,6},{6,5},{9,10},{10,9},{13,14},{14,13},{17,18},{18,... | collective-permute-start | bytes 3145736 | tf_op jit(solution)/shard_map/ppermute | solution.py:271
  5.3 33.3 %collective-permute-start = (bf16[4,1024,128]{2,1,0:T(8,128)(2,1)}, bf16[4,1024,128]{2,1,0:T(8,128)(2,1)}, u32[]{:S(2)}, u32[]{:S(2)}) collective-permute-start(bf16[4,1024,128]{2,1,0:T(8,128)(2,1)} %pad_maximum_fusion), channel_id=1, source_target_pairs={{0,1},{3,2},{4,5},{7,6},{8,9},{11,10},{12,13},{15,14},{16,17},{19,... | collective-permute-start | bytes 3145736 | tf_op jit(solution)/shard_map/ppermute | solution.py:270
  18.2 41.1 %collective-permute-start.1 = (bf16[4,1024,128]{2,1,0:T(8,128)(2,1)}, bf16[4,1024,128]{2,1,0:T(8,128)(2,1)}, u32[]{:S(2)}, u32[]{:S(2)}) collective-permute-start(bf16[4,1024,128]{2,1,0:T(8,128)(2,1)} %pad_maximum_fusion.1), channel_id=1, source_target_pairs={{0,1},{3,2},{4,5},{7,6},{8,9},{11,10},{12,13},{15,14},{16,17},{19,... | collective-permute-start | bytes 3145736 | tf_op jit(solution)/shard_map/ppermute | solution.py:274
  20.8 61.0 %collective-permute-start.8 = (bf16[1024,512]{1,0:T(8,128)(2,1)S(1)}, bf16[1024,512]{1,0:T(8,128)(2,1)S(1)}, u32[]{:S(2)}, u32[]{:S(2)}) collective-permute-start(bf16[1024,512]{1,0:T(8,128)(2,1)S(1)} %get-tuple-element.21), channel_id=1, source_target_pairs={{0,1},{3,2},{4,5},{7,6},{8,9},{11,10},{12,13},{15,14},{16,17},{19,... | collective-permute-start | bytes 3145736 | tf_op jit(solution)/shard_map/ppermute | solution.py:274
  22.3 62.1 %collective-permute-start.10 = (bf16[1024,512]{1,0:T(8,128)(2,1)S(1)}, bf16[1024,512]{1,0:T(8,128)(2,1)S(1)}, u32[]{:S(2)}, u32[]{:S(2)}) collective-permute-start(bf16[1024,512]{1,0:T(8,128)(2,1)S(1)} %get-tuple-element.22), channel_id=1, source_target_pairs={{1,2},{2,1},{5,6},{6,5},{9,10},{10,9},{13,14},{14,13},{17,18},{18,... | collective-permute-start | bytes 3145736 | tf_op jit(solution)/shard_map/ppermute | solution.py:271
  24.7 79.5 %collective-permute-start.6 = (bf16[1024,512]{1,0:T(8,128)(2,1)S(1)}, bf16[1024,512]{1,0:T(8,128)(2,1)}, u32[]{:S(2)}, u32[]{:S(2)}) collective-permute-start(bf16[1024,512]{1,0:T(8,128)(2,1)S(1)} %get-tuple-element.22), channel_id=1, source_target_pairs={{0,1},{3,2},{4,5},{7,6},{8,9},{11,10},{12,13},{15,14},{16,17},{19,... | collective-permute-start | bytes 3145736 | tf_op jit(solution)/shard_map/ppermute | solution.py:270
  38.7 86.7 %collective-permute-start.7 = (bf16[512,1024]{1,0:T(8,128)(2,1)}, bf16[512,1024]{1,0:T(8,128)(2,1)}, u32[]{:S(2)}, u32[]{:S(2)}) collective-permute-start(bf16[512,1024]{1,0:T(8,128)(2,1)} %get-tuple-element.20), channel_id=1, source_target_pairs={{0,1},{3,2},{4,5},{7,6},{8,9},{11,10},{12,13},{15,14},{16,17},{19,... | collective-permute-start | bytes 3145736 | tf_op jit(solution)/shard_map/ppermute | solution.py:270
  59.4 67.7 %collective-permute-start.4 = (bf16[4,1024,128]{2,1,0:T(8,128)(2,1)}, bf16[4,1024,128]{2,1,0:T(8,128)(2,1)}, u32[]{:S(2)}, u32[]{:S(2)}) collective-permute-start(bf16[4,1024,128]{2,1,0:T(8,128)(2,1)} %collective-permute-done.refs_6_), channel_id=1, source_target_pairs={{1,2},{2,1},{5,6},{6,5},{9,10},{10,9},{13,14},{14,13},{17,18},{18,... | collective-permute-start | bytes 3145736 | tf_op jit(solution)/shard_map/ppermute | solution.py:284
  82.7 46.0 %collective-permute-start.11 = (bf16[512,1024]{1,0:T(8,128)(2,1)}, bf16[512,1024]{1,0:T(8,128)(2,1)}, u32[]{:S(2)}, u32[]{:S(2)}) collective-permute-start(bf16[512,1024]{1,0:T(8,128)(2,1)} %get-tuple-element.20), channel_id=1, source_target_pairs={{1,2},{2,1},{5,6},{6,5},{9,10},{10,9},{13,14},{14,13},{17,18},{18,... | collective-permute-start | bytes 3145736 | tf_op jit(solution)/shard_map/ppermute | solution.py:271
  84.4 50.4 %collective-permute-start.3 = (bf16[4,1024,128]{2,1,0:T(8,128)(2,1)S(1)}, bf16[4,1024,128]{2,1,0:T(8,128)(2,1)}, u32[]{:S(2)}, u32[]{:S(2)}) collective-permute-start(bf16[4,1024,128]{2,1,0:T(8,128)(2,1)S(1)} %collective-permute-done.2.refs_8_), channel_id=1, source_target_pairs={{0,16},{16,0},{1,17},{17,1},{2,18},{18,2},{3,19},{19,3},{4,20},{20... | collective-permute-start | bytes 3145736 | tf_op jit(solution)/shard_map/ppermute | solution.py:278
  104.2 31.1 %collective-permute-start.14 = (bf16[1024,512]{1,0:T(8,128)(2,1)}, bf16[1024,512]{1,0:T(8,128)(2,1)}, u32[]{:S(2)}, u32[]{:S(2)}) collective-permute-start(bf16[1024,512]{1,0:T(8,128)(2,1)} %collective-permute-done.6.refs_2_), channel_id=1, source_target_pairs={{1,2},{2,1},{5,6},{6,5},{9,10},{10,9},{13,14},{14,13},{17,18},{18,... | collective-permute-start | bytes 3145736 | tf_op jit(solution)/shard_map/ppermute | solution.py:284
  125.4 11.4 %collective-permute-start.15 = (bf16[512,1024]{1,0:T(8,128)(2,1)}, bf16[512,1024]{1,0:T(8,128)(2,1)}, u32[]{:S(2)}, u32[]{:S(2)}) collective-permute-start(bf16[512,1024]{1,0:T(8,128)(2,1)} %collective-permute-done.7.refs_3_), channel_id=1, source_target_pairs={{1,2},{2,1},{5,6},{6,5},{9,10},{10,9},{13,14},{14,13},{17,18},{18,... | collective-permute-start | bytes 3145736 | tf_op jit(solution)/shard_map/ppermute | solution.py:284
  127.1 26.3 %collective-permute-start.5 = (bf16[4,1024,128]{2,1,0:T(8,128)(2,1)}, bf16[4,1024,128]{2,1,0:T(8,128)(2,1)}, u32[]{:S(2)}, u32[]{:S(2)}) collective-permute-start(bf16[4,1024,128]{2,1,0:T(8,128)(2,1)} %collective-permute-done.4.refs_10_), channel_id=1, source_target_pairs={{0,16},{16,0},{1,17},{17,1},{2,18},{18,2},{3,19},{19,3},{4,20},{20... | collective-permute-start | bytes 3145736 | tf_op jit(solution)/shard_map/ppermute | solution.py:278
  128.7 30.0 %collective-permute-start.9 = (bf16[512,1024]{1,0:T(8,128)(2,1)}, bf16[512,1024]{1,0:T(8,128)(2,1)}, u32[]{:S(2)}, u32[]{:S(2)}) collective-permute-start(bf16[512,1024]{1,0:T(8,128)(2,1)} %get-tuple-element.19), channel_id=1, source_target_pairs={{0,1},{3,2},{4,5},{7,6},{8,9},{11,10},{12,13},{15,14},{16,17},{19,... | collective-permute-start | bytes 3145736 | tf_op jit(solution)/shard_map/ppermute | solution.py:274
  134.8 41.1 %collective-permute-start.12 = (bf16[1024,512]{1,0:T(8,128)(2,1)}, bf16[1024,512]{1,0:T(8,128)(2,1)}, u32[]{:S(2)}, u32[]{:S(2)}) collective-permute-start(bf16[1024,512]{1,0:T(8,128)(2,1)} %copy-done.17), channel_id=1, source_target_pairs={{0,16},{16,0},{1,17},{17,1},{2,18},{18,2},{3,19},{19,3},{4,20},{20... | collective-permute-start | bytes 3145736 | tf_op jit(solution)/shard_map/ppermute | solution.py:278
  135.3 63.1 %collective-permute-start.13 = (bf16[512,1024]{1,0:T(8,128)(2,1)}, bf16[512,1024]{1,0:T(8,128)(2,1)}, u32[]{:S(2)}, u32[]{:S(2)}) collective-permute-start(bf16[512,1024]{1,0:T(8,128)(2,1)} %collective-permute-done.11.refs_7_), channel_id=1, source_target_pairs={{0,16},{16,0},{1,17},{17,1},{2,18},{18,2},{3,19},{19,3},{4,20},{20... | collective-permute-start | bytes 3145736 | tf_op jit(solution)/shard_map/ppermute | solution.py:278
  136.8 84.1 %collective-permute-start.16 = (bf16[1024,512]{1,0:T(8,128)(2,1)}, bf16[1024,512]{1,0:T(8,128)(2,1)}, u32[]{:S(2)}, u32[]{:S(2)}) collective-permute-start(bf16[1024,512]{1,0:T(8,128)(2,1)} %collective-permute-done.14.refs_10_), channel_id=1, source_target_pairs={{0,16},{16,0},{1,17},{17,1},{2,18},{18,2},{3,19},{19,3},{4,20},{20... | collective-permute-start | bytes 3145736 | tf_op jit(solution)/shard_map/ppermute | solution.py:278
  153.5 87.6 %collective-permute-start.17 = (bf16[512,1024]{1,0:T(8,128)(2,1)}, bf16[512,1024]{1,0:T(8,128)(2,1)}, u32[]{:S(2)}, u32[]{:S(2)}) collective-permute-start(bf16[512,1024]{1,0:T(8,128)(2,1)} %collective-permute-done.15.refs_11_), channel_id=1, source_target_pairs={{0,16},{16,0},{1,17},{17,1},{2,18},{18,2},{3,19},{19,3},{4,20},{20... | collective-permute-start | bytes 3145736 | tf_op jit(solution)/shard_map/ppermute | solution.py:278
  242.4 3.6 collective-permute-start.18
  254.6 4.6 %collective-permute-start.21 = (bf16[512,1024]{1,0:T(8,128)(2,1)S(1)}, bf16[512,1024]{1,0:T(8,128)(2,1)S(1)}, u32[]{:S(2)}, u32[]{:S(2)}) collective-permute-start(bf16[512,1024]{1,0:T(8,128)(2,1)S(1)} %get-tuple-element.11), channel_id=1, source_target_pairs={{0,4},{1,5},{2,6},{3,7},{16,20},{17,21},{18,22},{19,23}} | collective-permute-start | bytes 3145736 | tf_op jit(solution)/shard_map/ppermute | solution.py:336
  257.0 5.4 %collective-permute-start.19 = (bf16[512,1024]{1,0:T(8,128)(2,1)S(1)}, bf16[512,1024]{1,0:T(8,128)(2,1)S(1)}, u32[]{:S(2)}, u32[]{:S(2)}) collective-permute-start(bf16[512,1024]{1,0:T(8,128)(2,1)S(1)} %get-tuple-element.11), channel_id=1, source_target_pairs={{4,8},{5,9},{6,10},{7,11},{20,24},{21,25},{22,26},{23,27}} | collective-permute-start | bytes 3145736 | tf_op jit(solution)/shard_map/ppermute | solution.py:336
  261.6 10.0 %collective-permute-start.22 = (bf16[512,1024]{1,0:T(8,128)(2,1)}, bf16[512,1024]{1,0:T(8,128)(2,1)S(1)}, u32[]{:S(2)}, u32[]{:S(2)}) collective-permute-start(bf16[512,1024]{1,0:T(8,128)(2,1)} %get-tuple-element.13), channel_id=1, source_target_pairs={{4,8},{5,9},{6,10},{7,11},{20,24},{21,25},{22,26},{23,27}} | collective-permute-start | bytes 3145736 | tf_op jit(solution)/shard_map/ppermute | solution.py:336
  270.9 0.7 collective-permute-start.20
  274.1 1.7 collective-permute-start.23
  (21 other events, 738.8 us)
where the time goes:
time: 442 us; the launch traced here: 434 us
  waiting for transfers between devices  177 us (40%)
  blocking collectives  147 us (33%)
  starting transfers between devices  59.1 us (13%)
  Pallas kernels  29.1 us (7%)
  local copies, waits for them, and re-layouts  15.6 us (4%)
  other arithmetic  4.56 us (1%)
    psum x1, blocking collectives, per_device(): table = lax.psum(table, 'tensor').astype(jnp.bfloat16)  123 us
    ppermute x6, waiting for transfers between devices, pass_on(): swapped[index].append(lax.ppermute(crossed[index][kind], 'dp', swap))  98.5 us
    ppermute x3, waiting for transfers between devices, per_device(): seconds[index + 1].append(lax.ppermute(own_second[kind], 'tensor', pairs))  37.8 us
    ppermute x3, waiting for transfers between devices, per_device(): firsts[index + 1].append(lax.ppermute(own_first[kind], 'tensor', pairs))  36.9 us
    ppermute x3, starting transfers between devices, per_device(): firsts[index + 1].append(lax.ppermute(own_first[kind], 'tensor', pairs))  26.2 us
    psum x1, blocking collectives, per_device(): table = lax.psum(lax.all_gather(embedded, 'dp'), 'pipe')  19.8 us
    pallas_call x6, Pallas kernels, attention_half(): pl.pallas_call(functools.partial(attention_kernel, slot, shares, len(pass...  19.8 us
    ppermute x3, starting transfers between devices, per_device(): seconds[index + 1].append(lax.ppermute(own_second[kind], 'tensor', pairs))  9.84 us
  transfers between devices with their start and end apart: 24, of which 11 were waited for; matrix products, arithmetic and copies ran while one was open for 2% of the time, Pallas kernels for 3%

commit v1 on v0

--- a/solution.py
+++ b/solution.py
@@ -283,11 +283,9 @@
         for index in range(1, side):
             crossed[index].append(lax.ppermute(firsts[index][kind], "tensor", across))
         pass_on(0, kind)
-        if kind > 0:
-            for index in range(1, side):
-                pass_on(index, kind - 1)
-    for index in range(1, side):
-        pass_on(index, kinds - 1)
+    for kind in range(kinds):
+        for index in range(1, side):
+            pass_on(index, kind)
     halves = []
     for index in range(1, side):
         halves += [firsts[index], seconds[index]]

time: 442 us -> 442 us (level)
  no operation moved by 1% of the time
where the time goes in v1:
time: 442 us; the launch traced here: 434 us
  waiting for transfers between devices  177 us (40%)
  blocking collectives  147 us (33%)
  starting transfers between devices  59.1 us (13%)
  Pallas kernels  29.1 us (7%)
  local copies, waits for them, and re-layouts  15.6 us (4%)
  other arithmetic  4.56 us (1%)
    psum x1, blocking collectives, per_device(): table = lax.psum(table, 'tensor').astype(jnp.bfloat16)  123 us
    ppermute x6, waiting for transfers between devices, pass_on(): swapped[index].append(lax.ppermute(crossed[index][kind], 'dp', swap))  98.5 us
    ppermute x3, waiting for transfers between devices, per_device(): seconds[index + 1].append(lax.ppermute(own_second[kind], 'tensor', pairs))  37.8 us
    ppermute x3, waiting for transfers between devices, per_device(): firsts[index + 1].append(lax.ppermute(own_first[kind], 'tensor', pairs))  36.9 us
    ppermute x3, starting transfers between devices, per_device(): firsts[index + 1].append(lax.ppermute(own_first[kind], 'tensor', pairs))  26.2 us
    psum x1, blocking collectives, per_device(): table = lax.psum(lax.all_gather(embedded, 'dp'), 'pipe')  19.8 us
    pallas_call x6, Pallas kernels, attention_half(): pl.pallas_call(functools.partial(attention_kernel, slot, shares, len(pass...  19.8 us
    ppermute x3, starting transfers between devices, per_device(): seconds[index + 1].append(lax.ppermute(own_second[kind], 'tensor', pairs))  9.84 us
  transfers between devices with their start and end apart: 24, of which 11 were waited for; matrix products, arithmetic and copies ran while one was open for 2% of the time, Pallas kernels for 3%

profile of v1, /device:TPU:0, one launch (start us, length us, event | category | flops | bytes accessed | tf_op | source)
XLA Modules:
  0.0 433.6 jit_solution(11764018323223288510)
XLA Ops:
  5.3 8.7 %collective-permute-start = (bf16[4,1024,128]{2,1,0:T(8,128)(2,1)}, bf16[4,1024,128]{2,1,0:T(8,128)(2,1)}, u32[]{:S(2)}, u32[]{:S(2)}) collective-permute-start(bf16[4,1024,128]{2,1,0:T(8,128)(2,1)} %pad_maximum_fusion), channel_id=1, source_target_pairs={{0,1},{3,2},{4,5},{7,6},{8,9},{11,10},{12,13},{15,14},{16,17},{19,... | collective-permute-start | bytes 3145736 | tf_op jit(solution)/shard_map/ppermute | solution.py:270
  16.0 2.2 pad_maximum_fusion.1
  18.2 2.3 collective-permute-start.1
  24.7 13.9 %collective-permute-start.6 = (bf16[1024,512]{1,0:T(8,128)(2,1)S(1)}, bf16[1024,512]{1,0:T(8,128)(2,1)}, u32[]{:S(2)}, u32[]{:S(2)}) collective-permute-start(bf16[1024,512]{1,0:T(8,128)(2,1)S(1)} %get-tuple-element.22), channel_id=1, source_target_pairs={{0,1},{3,2},{4,5},{7,6},{8,9},{11,10},{12,13},{15,14},{16,17},{19,... | collective-permute-start | bytes 3145736 | tf_op jit(solution)/shard_map/ppermute | solution.py:270
  38.7 3.6 collective-permute-start.7
  42.3 17.1 %collective-permute-done.1.refs_7_ = bf16[4,1024,128]{2,1,0:T(8,128)(2,1)} collective-permute-done((bf16[4,1024,128]{2,1,0:T(8,128)(2,1)}, bf16[4,1024,128]{2,1,0:T(8,128)(2,1)}, u32[]{:S(2)}, u32[]{:S(2)}) %collective-permute-start.1) | collective-permute-done | bytes 1048608 | tf_op jit(solution)/shard_map/ppermute | solution.py:274
  61.0 20.7 %collective-permute-done.8.refs_4_ = bf16[1024,512]{1,0:T(8,128)(2,1)S(1)} collective-permute-done((bf16[1024,512]{1,0:T(8,128)(2,1)S(1)}, bf16[1024,512]{1,0:T(8,128)(2,1)S(1)}, u32[]{:S(2)}, u32[]{:S(2)}) %collective-permute-start.8) | collective-permute-done | bytes 1048608 | tf_op jit(solution)/shard_map/ppermute | solution.py:274
  86.9 17.3 %collective-permute-done.6.refs_2_ = bf16[1024,512]{1,0:T(8,128)(2,1)} collective-permute-done((bf16[1024,512]{1,0:T(8,128)(2,1)S(1)}, bf16[1024,512]{1,0:T(8,128)(2,1)}, u32[]{:S(2)}, u32[]{:S(2)}) %collective-permute-start.6) | collective-permute-done | bytes 1048608 | tf_op jit(solution)/shard_map/ppermute | solution.py:270
  105.8 19.5 %collective-permute-done.7.refs_3_ = bf16[512,1024]{1,0:T(8,128)(2,1)} collective-permute-done((bf16[512,1024]{1,0:T(8,128)(2,1)}, bf16[512,1024]{1,0:T(8,128)(2,1)}, u32[]{:S(2)}, u32[]{:S(2)}) %collective-permute-start.7) | collective-permute-done | bytes 1048608 | tf_op jit(solution)/shard_map/ppermute | solution.py:270
  128.7 6.1 %collective-permute-start.9 = (bf16[512,1024]{1,0:T(8,128)(2,1)}, bf16[512,1024]{1,0:T(8,128)(2,1)}, u32[]{:S(2)}, u32[]{:S(2)}) collective-permute-start(bf16[512,1024]{1,0:T(8,128)(2,1)} %get-tuple-element.19), channel_id=1, source_target_pairs={{0,1},{3,2},{4,5},{7,6},{8,9},{11,10},{12,13},{15,14},{16,17},{19,... | collective-permute-start | bytes 3145736 | tf_op jit(solution)/shard_map/ppermute | solution.py:274
  137.3 16.1 %collective-permute-done.5.refs_11_ = bf16[4,1024,128]{2,1,0:T(8,128)(2,1)} collective-permute-done((bf16[4,1024,128]{2,1,0:T(8,128)(2,1)}, bf16[4,1024,128]{2,1,0:T(8,128)(2,1)}, u32[]{:S(2)}, u32[]{:S(2)}) %collective-permute-start.5) | collective-permute-done | bytes 1048608 | tf_op jit(solution)/shard_map/ppermute | solution.py:278
  158.7 17.2 %collective-permute-done.12.refs_8_ = bf16[1024,512]{1,0:T(8,128)(2,1)} collective-permute-done((bf16[1024,512]{1,0:T(8,128)(2,1)}, bf16[1024,512]{1,0:T(8,128)(2,1)}, u32[]{:S(2)}, u32[]{:S(2)}) %collective-permute-start.12) | collective-permute-done | bytes 1048608 | tf_op jit(solution)/shard_map/ppermute | solution.py:278
  175.9 22.5 %collective-permute-done.13.refs_9_ = bf16[512,1024]{1,0:T(8,128)(2,1)} collective-permute-done((bf16[512,1024]{1,0:T(8,128)(2,1)}, bf16[512,1024]{1,0:T(8,128)(2,1)}, u32[]{:S(2)}, u32[]{:S(2)}) %collective-permute-start.13) | collective-permute-done | bytes 1048608 | tf_op jit(solution)/shard_map/ppermute | solution.py:278
  198.4 22.5 %collective-permute-done.16.refs_12_ = bf16[1024,512]{1,0:T(8,128)(2,1)} collective-permute-done((bf16[1024,512]{1,0:T(8,128)(2,1)}, bf16[1024,512]{1,0:T(8,128)(2,1)}, u32[]{:S(2)}, u32[]{:S(2)}) %collective-permute-start.16) | collective-permute-done | bytes 1048608 | tf_op jit(solution)/shard_map/ppermute | solution.py:278
  220.9 20.2 %collective-permute-done.17.refs_13_ = bf16[512,1024]{1,0:T(8,128)(2,1)} collective-permute-done((bf16[512,1024]{1,0:T(8,128)(2,1)}, bf16[512,1024]{1,0:T(8,128)(2,1)}, u32[]{:S(2)}, u32[]{:S(2)}) %collective-permute-start.17) | collective-permute-done | bytes 1048608 | tf_op jit(solution)/shard_map/ppermute | solution.py:278
  243.8 2.2 collective-permute-done.18.refs_2_
  246.0 7.2 %attention_half.7.hidden = bf16[512,1024]{1,0:T(8,128)(2,1)S(1)} custom-call(s32[6,4]{1,0:T(8,128)S(1)} %pad_add_fusion.plan, bf16[2,512,1024]{2,1,0:T(8,128)(2,1)S(1)} %copy-done, bf16[2,512,1024]{2,1,0:T(8,128)(2,1)} %refs_1_.11, bf16[512,1024]{1,0:T(8,128)(2,1)S(1)} %collective-permute-done.18.refs_2_, ...), custom_call_target="tpu_custom_call" | custom-call | tf_op jit(solution)/shard_map/attention_half/pallas_call | solution.py:133
  254.6 2.3 collective-permute-start.21
  262.4 7.1 %attention_half.8.hidden = bf16[512,1024]{1,0:T(8,128)(2,1)S(1)} custom-call(s32[6,4]{1,0:T(8,128)S(1)} %pad_add_fusion.plan, bf16[2,512,1024]{2,1,0:T(8,128)(2,1)S(1)} %copy-done, bf16[2,512,1024]{2,1,0:T(8,128)(2,1)} %refs_1_.11, bf16[512,1024]{1,0:T(8,128)(2,1)S(1)} %slice_bitcast_fusion.refs_2_.refs_3_, ...), custom_call_target="tpu_custom_call" | custom-call | tf_op jit(solution)/shard_map/attention_half/pallas_call | solution.py:133
  272.3 1.8 mlp_half.10
  279.5 3.4 attention_half.11.hidden
  285.0 4.4 %all_gather.4 = bf16[2,2,1024]{2,1,0:T(2,128)(2,1)S(1)} all-gather(bf16[1,2,1024]{2,1,0:T(2,128)(2,1)S(1)} %broadcast_select_fusion.1), channel_id=1, replica_groups=mesh['dp'=2,'pipe'=4,'tensor'=4] {'dp'}, dimensions={0}, use_global_device_ids=true | all-gather | bytes 12288 | tf_op jit(solution)/shard_map/all_gather | solution.py:343
  289.3 19.8 %psum.14 = bf16[2,2,1024]{2,1,0:T(2,128)(2,1)S(1)} all-reduce(bf16[2,2,1024]{2,1,0:T(2,128)(2,1)S(1)} %all_gather.4), channel_id=1, replica_groups=mesh['dp'=2,'pipe'=4,'tensor'=4] {'pipe'}, use_global_device_ids=true, to_apply=%region_2.3 | all-reduce | flops 4096 | bytes 16384 | tf_op jit(solution)/shard_map/psum | solution.py:343
  309.3 122.7 %psum.15 = bf16[2,4,1024]{2,1,0:T(4,128)(2,1)S(1)} all-reduce(bf16[2,4,1024]{2,1,0:T(4,128)(2,1)S(1)} %reshape.167), channel_id=1, replica_groups=mesh['dp'=2,'pipe'=4,'tensor'=4] {'tensor'}, use_global_device_ids=true, to_apply=%region_3.4 | all-reduce | flops 8192 | bytes 32768 | tf_op jit(solution)/shard_map/psum | solution.py:349
  (113 shorter events, 51.4 us)
Async XLA Ops:
  4.5 20.3 %collective-permute-start.2 = (bf16[4,1024,128]{2,1,0:T(8,128)(2,1)}, bf16[4,1024,128]{2,1,0:T(8,128)(2,1)S(1)}, u32[]{:S(2)}, u32[]{:S(2)}) collective-permute-start(bf16[4,1024,128]{2,1,0:T(8,128)(2,1)} %pad_maximum_fusion), channel_id=1, source_target_pairs={{1,2},{2,1},{5,6},{6,5},{9,10},{10,9},{13,14},{14,13},{17,18},{18,... | collective-permute-start | bytes 3145736 | tf_op jit(solution)/shard_map/ppermute | solution.py:271
  5.3 33.3 %collective-permute-start = (bf16[4,1024,128]{2,1,0:T(8,128)(2,1)}, bf16[4,1024,128]{2,1,0:T(8,128)(2,1)}, u32[]{:S(2)}, u32[]{:S(2)}) collective-permute-start(bf16[4,1024,128]{2,1,0:T(8,128)(2,1)} %pad_maximum_fusion), channel_id=1, source_target_pairs={{0,1},{3,2},{4,5},{7,6},{8,9},{11,10},{12,13},{15,14},{16,17},{19,... | collective-permute-start | bytes 3145736 | tf_op jit(solution)/shard_map/ppermute | solution.py:270
  18.2 41.1 %collective-permute-start.1 = (bf16[4,1024,128]{2,1,0:T(8,128)(2,1)}, bf16[4,1024,128]{2,1,0:T(8,128)(2,1)}, u32[]{:S(2)}, u32[]{:S(2)}) collective-permute-start(bf16[4,1024,128]{2,1,0:T(8,128)(2,1)} %pad_maximum_fusion.1), channel_id=1, source_target_pairs={{0,1},{3,2},{4,5},{7,6},{8,9},{11,10},{12,13},{15,14},{16,17},{19,... | collective-permute-start | bytes 3145736 | tf_op jit(solution)/shard_map/ppermute | solution.py:274
  20.8 61.0 %collective-permute-start.8 = (bf16[1024,512]{1,0:T(8,128)(2,1)S(1)}, bf16[1024,512]{1,0:T(8,128)(2,1)S(1)}, u32[]{:S(2)}, u32[]{:S(2)}) collective-permute-start(bf16[1024,512]{1,0:T(8,128)(2,1)S(1)} %get-tuple-element.21), channel_id=1, source_target_pairs={{0,1},{3,2},{4,5},{7,6},{8,9},{11,10},{12,13},{15,14},{16,17},{19,... | collective-permute-start | bytes 3145736 | tf_op jit(solution)/shard_map/ppermute | solution.py:274
  22.3 62.1 %collective-permute-start.10 = (bf16[1024,512]{1,0:T(8,128)(2,1)S(1)}, bf16[1024,512]{1,0:T(8,128)(2,1)S(1)}, u32[]{:S(2)}, u32[]{:S(2)}) collective-permute-start(bf16[1024,512]{1,0:T(8,128)(2,1)S(1)} %get-tuple-element.22), channel_id=1, source_target_pairs={{1,2},{2,1},{5,6},{6,5},{9,10},{10,9},{13,14},{14,13},{17,18},{18,... | collective-permute-start | bytes 3145736 | tf_op jit(solution)/shard_map/ppermute | solution.py:271
  24.7 79.5 %collective-permute-start.6 = (bf16[1024,512]{1,0:T(8,128)(2,1)S(1)}, bf16[1024,512]{1,0:T(8,128)(2,1)}, u32[]{:S(2)}, u32[]{:S(2)}) collective-permute-start(bf16[1024,512]{1,0:T(8,128)(2,1)S(1)} %get-tuple-element.22), channel_id=1, source_target_pairs={{0,1},{3,2},{4,5},{7,6},{8,9},{11,10},{12,13},{15,14},{16,17},{19,... | collective-permute-start | bytes 3145736 | tf_op jit(solution)/shard_map/ppermute | solution.py:270
  38.7 86.7 %collective-permute-start.7 = (bf16[512,1024]{1,0:T(8,128)(2,1)}, bf16[512,1024]{1,0:T(8,128)(2,1)}, u32[]{:S(2)}, u32[]{:S(2)}) collective-permute-start(bf16[512,1024]{1,0:T(8,128)(2,1)} %get-tuple-element.20), channel_id=1, source_target_pairs={{0,1},{3,2},{4,5},{7,6},{8,9},{11,10},{12,13},{15,14},{16,17},{19,... | collective-permute-start | bytes 3145736 | tf_op jit(solution)/shard_map/ppermute | solution.py:270
  59.4 67.7 %collective-permute-start.4 = (bf16[4,1024,128]{2,1,0:T(8,128)(2,1)}, bf16[4,1024,128]{2,1,0:T(8,128)(2,1)}, u32[]{:S(2)}, u32[]{:S(2)}) collective-permute-start(bf16[4,1024,128]{2,1,0:T(8,128)(2,1)} %collective-permute-done.refs_6_), channel_id=1, source_target_pairs={{1,2},{2,1},{5,6},{6,5},{9,10},{10,9},{13,14},{14,13},{17,18},{18,... | collective-permute-start | bytes 3145736 | tf_op jit(solution)/shard_map/ppermute | solution.py:284
  82.7 46.0 %collective-permute-start.11 = (bf16[512,1024]{1,0:T(8,128)(2,1)}, bf16[512,1024]{1,0:T(8,128)(2,1)}, u32[]{:S(2)}, u32[]{:S(2)}) collective-permute-start(bf16[512,1024]{1,0:T(8,128)(2,1)} %get-tuple-element.20), channel_id=1, source_target_pairs={{1,2},{2,1},{5,6},{6,5},{9,10},{10,9},{13,14},{14,13},{17,18},{18,... | collective-permute-start | bytes 3145736 | tf_op jit(solution)/shard_map/ppermute | solution.py:271
  84.4 50.4 %collective-permute-start.3 = (bf16[4,1024,128]{2,1,0:T(8,128)(2,1)S(1)}, bf16[4,1024,128]{2,1,0:T(8,128)(2,1)}, u32[]{:S(2)}, u32[]{:S(2)}) collective-permute-start(bf16[4,1024,128]{2,1,0:T(8,128)(2,1)S(1)} %collective-permute-done.2.refs_8_), channel_id=1, source_target_pairs={{0,16},{16,0},{1,17},{17,1},{2,18},{18,2},{3,19},{19,3},{4,20},{20... | collective-permute-start | bytes 3145736 | tf_op jit(solution)/shard_map/ppermute | solution.py:278
  104.2 31.1 %collective-permute-start.14 = (bf16[1024,512]{1,0:T(8,128)(2,1)}, bf16[1024,512]{1,0:T(8,128)(2,1)}, u32[]{:S(2)}, u32[]{:S(2)}) collective-permute-start(bf16[1024,512]{1,0:T(8,128)(2,1)} %collective-permute-done.6.refs_2_), channel_id=1, source_target_pairs={{1,2},{2,1},{5,6},{6,5},{9,10},{10,9},{13,14},{14,13},{17,18},{18,... | collective-permute-start | bytes 3145736 | tf_op jit(solution)/shard_map/ppermute | solution.py:284
  125.4 11.4 %collective-permute-start.15 = (bf16[512,1024]{1,0:T(8,128)(2,1)}, bf16[512,1024]{1,0:T(8,128)(2,1)}, u32[]{:S(2)}, u32[]{:S(2)}) collective-permute-start(bf16[512,1024]{1,0:T(8,128)(2,1)} %collective-permute-done.7.refs_3_), channel_id=1, source_target_pairs={{1,2},{2,1},{5,6},{6,5},{9,10},{10,9},{13,14},{14,13},{17,18},{18,... | collective-permute-start | bytes 3145736 | tf_op jit(solution)/shard_map/ppermute | solution.py:284
  127.1 26.3 %collective-permute-start.5 = (bf16[4,1024,128]{2,1,0:T(8,128)(2,1)}, bf16[4,1024,128]{2,1,0:T(8,128)(2,1)}, u32[]{:S(2)}, u32[]{:S(2)}) collective-permute-start(bf16[4,1024,128]{2,1,0:T(8,128)(2,1)} %collective-permute-done.4.refs_10_), channel_id=1, source_target_pairs={{0,16},{16,0},{1,17},{17,1},{2,18},{18,2},{3,19},{19,3},{4,20},{20... | collective-permute-start | bytes 3145736 | tf_op jit(solution)/shard_map/ppermute | solution.py:278
  128.7 30.0 %collective-permute-start.9 = (bf16[512,1024]{1,0:T(8,128)(2,1)}, bf16[512,1024]{1,0:T(8,128)(2,1)}, u32[]{:S(2)}, u32[]{:S(2)}) collective-permute-start(bf16[512,1024]{1,0:T(8,128)(2,1)} %get-tuple-element.19), channel_id=1, source_target_pairs={{0,1},{3,2},{4,5},{7,6},{8,9},{11,10},{12,13},{15,14},{16,17},{19,... | collective-permute-start | bytes 3145736 | tf_op jit(solution)/shard_map/ppermute | solution.py:274
  134.8 41.1 %collective-permute-start.12 = (bf16[1024,512]{1,0:T(8,128)(2,1)}, bf16[1024,512]{1,0:T(8,128)(2,1)}, u32[]{:S(2)}, u32[]{:S(2)}) collective-permute-start(bf16[1024,512]{1,0:T(8,128)(2,1)} %copy-done.17), channel_id=1, source_target_pairs={{0,16},{16,0},{1,17},{17,1},{2,18},{18,2},{3,19},{19,3},{4,20},{20... | collective-permute-start | bytes 3145736 | tf_op jit(solution)/shard_map/ppermute | solution.py:278
  135.3 63.1 %collective-permute-start.13 = (bf16[512,1024]{1,0:T(8,128)(2,1)}, bf16[512,1024]{1,0:T(8,128)(2,1)}, u32[]{:S(2)}, u32[]{:S(2)}) collective-permute-start(bf16[512,1024]{1,0:T(8,128)(2,1)} %collective-permute-done.11.refs_7_), channel_id=1, source_target_pairs={{0,16},{16,0},{1,17},{17,1},{2,18},{18,2},{3,19},{19,3},{4,20},{20... | collective-permute-start | bytes 3145736 | tf_op jit(solution)/shard_map/ppermute | solution.py:278
  136.8 84.1 %collective-permute-start.16 = (bf16[1024,512]{1,0:T(8,128)(2,1)}, bf16[1024,512]{1,0:T(8,128)(2,1)}, u32[]{:S(2)}, u32[]{:S(2)}) collective-permute-start(bf16[1024,512]{1,0:T(8,128)(2,1)} %collective-permute-done.14.refs_10_), channel_id=1, source_target_pairs={{0,16},{16,0},{1,17},{17,1},{2,18},{18,2},{3,19},{19,3},{4,20},{20... | collective-permute-start | bytes 3145736 | tf_op jit(solution)/shard_map/ppermute | solution.py:278
  153.5 87.6 %collective-permute-start.17 = (bf16[512,1024]{1,0:T(8,128)(2,1)}, bf16[512,1024]{1,0:T(8,128)(2,1)}, u32[]{:S(2)}, u32[]{:S(2)}) collective-permute-start(bf16[512,1024]{1,0:T(8,128)(2,1)} %collective-permute-done.15.refs_11_), channel_id=1, source_target_pairs={{0,16},{16,0},{1,17},{17,1},{2,18},{18,2},{3,19},{19,3},{4,20},{20... | collective-permute-start | bytes 3145736 | tf_op jit(solution)/shard_map/ppermute | solution.py:278
  242.4 3.6 collective-permute-start.18
  254.6 4.6 %collective-permute-start.21 = (bf16[512,1024]{1,0:T(8,128)(2,1)S(1)}, bf16[512,1024]{1,0:T(8,128)(2,1)S(1)}, u32[]{:S(2)}, u32[]{:S(2)}) collective-permute-start(bf16[512,1024]{1,0:T(8,128)(2,1)S(1)} %get-tuple-element.11), channel_id=1, source_target_pairs={{0,4},{1,5},{2,6},{3,7},{16,20},{17,21},{18,22},{19,23}} | collective-permute-start | bytes 3145736 | tf_op jit(solution)/shard_map/ppermute | solution.py:334
  257.0 5.4 %collective-permute-start.19 = (bf16[512,1024]{1,0:T(8,128)(2,1)S(1)}, bf16[512,1024]{1,0:T(8,128)(2,1)S(1)}, u32[]{:S(2)}, u32[]{:S(2)}) collective-permute-start(bf16[512,1024]{1,0:T(8,128)(2,1)S(1)} %get-tuple-element.11), channel_id=1, source_target_pairs={{4,8},{5,9},{6,10},{7,11},{20,24},{21,25},{22,26},{23,27}} | collective-permute-start | bytes 3145736 | tf_op jit(solution)/shard_map/ppermute | solution.py:334
  261.6 10.0 %collective-permute-start.22 = (bf16[512,1024]{1,0:T(8,128)(2,1)}, bf16[512,1024]{1,0:T(8,128)(2,1)S(1)}, u32[]{:S(2)}, u32[]{:S(2)}) collective-permute-start(bf16[512,1024]{1,0:T(8,128)(2,1)} %get-tuple-element.13), channel_id=1, source_target_pairs={{4,8},{5,9},{6,10},{7,11},{20,24},{21,25},{22,26},{23,27}} | collective-permute-start | bytes 3145736 | tf_op jit(solution)/shard_map/ppermute | solution.py:334
  270.9 0.7 collective-permute-start.20
  274.1 1.7 collective-permute-start.23
  (21 other events, 738.8 us)
